TPU v7x, 32 devices: a whole 2x2x4 slice. The times are simulated.
32 devices in a mesh: ta: 4 (over x, core), tb: 8 (over z, y).
Axes of the slice: x: 2, y: 2, z: 4, core: 2. Of those that a mesh axis runs over, the one named last changes fastest.
Arguments:
- theta_cube: bfloat16 [32, 90, 4096], P(('ta', 'tb')), may hold values from -20 to 20, as said below
- station_permutation_map: int32 [128], replicated, may hold values from 0 to 127, each once
- station_bathymetry_group: int32 [4096], replicated, may hold values from 0 to 15
- baroclinic_basis: bfloat16 [16, 90, 90], replicated, may hold values from -0.625 to 0.625
Outputs:
- anomaly_coef: bfloat16 [90, 32, 4096], P(None, None, ('ta', 'tb'))
Inputs may be any that keep to these rules, and one draw needn't show every extreme that they name: `theta_cube`: temperature is a level-and-column profile plus time variation.
All inputs are finite; a program needn't handle non-finite values.
Results may differ from a plain program's by a relative error of at most 0.001.
Values may be sent and summed in bfloat16 or wider, within the bound.
A program may use at most 128 MiB of HBM per device.

v0:
```python
import jax
import jax.numpy as jnp
from jax import lax
from jax.sharding import PartitionSpec as P

TILE = 32


def on_device(theta_cube, station_permutation_map, station_bathymetry_group, baroclinic_basis):
    instant_portion, vertical_grid_count, ocean_stations = theta_cube.shape
    classes, _, mode_count = baroclinic_basis.shape
    size_ta = lax.axis_size("ta")
    size_tb = lax.axis_size("tb")
    devices = size_ta * size_tb
    col_dev = ocean_stations // devices
    group_count = ocean_stations // TILE
    owner = lax.axis_index("ta") * size_tb + lax.axis_index("tb")
    grouped = theta_cube.reshape(instant_portion, vertical_grid_count, group_count, TILE)
    regrouped_stations = jnp.take(grouped, station_permutation_map, axis=2).reshape(
        instant_portion, vertical_grid_count, devices, col_dev
    )
    my_groups = lax.dynamic_slice_in_dim(
        station_permutation_map, owner * (col_dev // TILE), col_dev // TILE
    )
    my_columns = (my_groups[:, None] * TILE + jnp.arange(TILE, dtype=jnp.int32)[None, :]).reshape(
        col_dev
    )
    local_category = jnp.take(station_bathymetry_group, my_columns, axis=0)
    one_hot = (local_category[:, None] == jnp.arange(classes, dtype=jnp.int32)[None, :]).astype(
        jnp.bfloat16
    )
    per_column = jnp.dot(
        one_hot,
        baroclinic_basis.reshape(classes, vertical_grid_count * mode_count),
        preferred_element_type=jnp.float32,
    )
    per_column = per_column.astype(jnp.bfloat16).reshape(col_dev, vertical_grid_count, mode_count)
    shaped = regrouped_stations.reshape(
        1, 1, instant_portion, vertical_grid_count, size_ta, size_tb, col_dev
    )
    moved = lax.all_to_all(
        lax.all_to_all(shaped, "ta", split_axis=4, concat_axis=0, tiled=True),
        "tb",
        split_axis=5,
        concat_axis=1,
        tiled=True,
    )
    gathered = moved.reshape(devices * instant_portion, vertical_grid_count, col_dev)
    modal_amplitude = jnp.einsum(
        "btq,qtf->fbq", gathered, per_column, preferred_element_type=jnp.float32
    )
    mean_coef = jnp.mean(modal_amplitude, axis=1, keepdims=True)
    return (modal_amplitude - mean_coef).astype(jnp.bfloat16)


def solution(mesh):
    return jax.shard_map(
        on_device,
        mesh=mesh,
        in_specs=(P(("ta", "tb"), None, None), P(), P(), P()),
        out_specs=P(None, None, ("ta", "tb")),
        check_vma=False,
    )
```

profile of v0, /device:TPU:0, one launch (start us, length us, event | category | flops | bytes accessed | tf_op | source)
XLA Modules:
  0.0 55.1 jit_solution(2020896969279646395)
XLA Ops:
  0.0 0.0 copy-start
  0.0 0.7 %compare_select_fusion = s32[128]{0:T(128)S(1)} fusion(s32[128]{0:T(128)} %param.5), kind=kLoop, calls=%fused_computation.14 | loop fusion | flops 384 | bytes 1024 | tf_op jit(solution)/shard_map/jit(_take)/jit(_where)/select_n | solution.py:19
  0.7 0.7 %compare_and_fusion = pred[128]{0:T(512)(128)(4,1)S(1)} fusion(s32[128]{0:T(128)} %param.5), kind=kLoop, calls=%fused_computation.18 | loop fusion | flops 768 | bytes 640 | tf_op jit(solution)/shard_map/jit(_take)/and | solution.py:19
  1.3 1.6 %copy.14 = bf16[1,90,4096]{1,2,0:T(8,128)(2,1)S(1)} copy(bf16[1,90,4096]{2,1,0:T(8,128)(2,1)} %param.4) | data formatting | bytes 1474560 | tf_op args[0]
  2.9 0.1 broadcast_in_dim.30
  3.1 0.1 broadcast_in_dim.31
  3.2 0.1 broadcast_in_dim.32
  3.3 0.8 %gather_fusion.1 = bf16[128,90,32]{1,2,0:T(8,128)(2,1)S(1)} fusion(bf16[90,128,32]{0,2,1:T(8,128)(2,1)S(1)} %bitcast.28, s32[1024]{0:T(1024)S(1)} %pad_clamp_fusion), kind=kCustom, calls=%fused_computation.1 | custom fusion | bytes 1475072 | tf_op jit(solution)/shard_map/jit(_take)/gather | solution.py:19
  4.0 0.7 %broadcast_select_fusion = bf16[1,1,1,90,4,8,128]{3,6,5,4,2,1,0:T(8,128)(2,1)S(1)} fusion(bf16[1,1,1,90,4,8,128]{3,6,5,4,2,1,0:T(8,128)(2,1)S(1)} %bitcast.29, pred[4,8,128]{2,1,0:T(8,128)(4,1)S(1)} %broadcast_in_dim.32), kind=kLoop, calls=%fused_computation.8 | loop fusion | flops 368640 | bytes 1478656 | tf_op jit(solution)/shard_map/jit(_take)/select_n | solution.py:19
  4.8 0.7 %copy.15 = bf16[1,1,1,90,4,8,128]{6,5,3,2,1,0,4:T(8,128)(2,1)S(1)} copy(bf16[1,1,1,90,4,8,128]{3,6,5,4,2,1,0:T(8,128)(2,1)S(1)} %broadcast_select_fusion) | data formatting | bytes 1474560 | tf_op jit(solution)/shard_map/jit(_take)/select_n | solution.py:19
  5.4 0.0 copy-start.2
  5.5 0.0 copy-start.1
  5.5 15.3 %all_to_all.33 = bf16[1,1,1,90,4,8,128]{6,5,3,2,1,0,4:T(8,128)(2,1)S(1)} all-to-all(bf16[1,1,1,90,4,8,128]{6,5,3,2,1,0,4:T(8,128)(2,1)S(1)} %copy.15), channel_id=1, replica_groups=mesh['ta'=4,'tb'=8] {'ta'}, dimensions={4} | all-to-all | bytes 1474560 | tf_op jit(solution)/shard_map/all_to_all | solution.py:42
  20.7 1.1 %copy.16 = bf16[4,1,1,90,1,8,128]{6,0,4,3,2,1,5:T(4,128)(2,1)} copy(bf16[4,1,1,90,1,8,128]{6,5,3,0,4,2,1:T(8,128)(2,1)S(1)} %bitcast.30) | data formatting | bytes 1474560 | tf_op jit(solution)/shard_map/all_to_all | solution.py:42
  21.9 5.8 %all-to-all-start.1 = ((bf16[4,1,1,90,1,8,128]{6,0,4,3,2,1,5:T(4,128)(2,1)}), bf16[4,1,1,90,1,8,128]{6,0,4,3,2,1,5:T(4,128)(2,1)}, u32[]{:S(2)}, u32[]{:S(2)}) async-start(bf16[4,1,1,90,1,8,128]{6,0,4,3,2,1,5:T(4,128)(2,1)} %copy.16), calls=%async_computation.1 | async-start | bytes 1474560 | tf_op jit(solution)/shard_map/all_to_all | solution.py:41
  27.7 0.0 copy-done.2
  27.7 0.1 dynamic-slice_multiply_fusion
  27.8 0.1 iota_add_fusion
  27.9 0.1 add.78
  28.0 0.1 add.75
  28.0 0.0 copy-done.1
  28.0 0.1 copy.13
  28.2 0.5 reshape.91
  28.7 0.0 copy-done
  28.7 1.1 %gather_fusion = s32[128]{0:T(128)S(1)} fusion(s32[4096]{0:T(1024)S(1)} %copy-done, s32[1024]{0:T(1024)S(1)} %pad_clamp_fusion.1), kind=kCustom, calls=%fused_computation | custom fusion | bytes 1536 | tf_op jit(solution)/shard_map/jit(_take)/gather | solution.py:28
  29.8 1.3 %convolution_convert_fusion = bf16[128,8100]{0,1:T(8,128)(2,1)S(1)} fusion(bf16[16,8100]{1,0:T(8,128)(2,1)S(1)} %reshape.91, s32[128]{0:T(128)S(1)} %and_select_fusion), kind=kOutput, calls=%fused_computation.2 | convolution fusion | flops 34216448 | bytes 2333312 | tf_op jit(solution)/shard_map/dot_general | solution.py:32
  31.2 1.9 %reshape.92 = bf16[128,90,90]{0,2,1:T(8,128)(2,1)} reshape(bf16[128,8100]{0,1:T(8,128)(2,1)S(1)} %convolution_convert_fusion) | data formatting | bytes 4147200 | tf_op jit(solution)/shard_map/reshape | solution.py:37
  33.1 3.6 %copy.18 = bf16[128,90,90]{2,1,0:T(8,128)(2,1)S(1)} copy(bf16[128,90,90]{0,2,1:T(8,128)(2,1)} %reshape.92) | data formatting | bytes 4147200 | tf_op jit(solution)/shard_map/reshape | solution.py:37
  36.7 10.1 %all-to-all-done.1 = bf16[4,1,1,90,1,8,128]{6,0,4,3,2,1,5:T(4,128)(2,1)} async-done(((bf16[4,1,1,90,1,8,128]{6,0,4,3,2,1,5:T(4,128)(2,1)}), bf16[4,1,1,90,1,8,128]{6,0,4,3,2,1,5:T(4,128)(2,1)}, u32[]{:S(2)}, u32[]{:S(2)}) %all-to-all-start.1) | async-done | bytes 737312 | tf_op jit(solution)/shard_map/all_to_all | solution.py:41
  46.8 3.7 %copy.17 = bf16[4,8,1,1,90,1,1,128]{4,1,0,7,6,5,3,2:T(8,128)(2,1)} copy(bf16[4,8,1,1,90,1,1,128]{7,0,4,1,6,5,3,2:T(4,128)(2,1)} %bitcast.8) | data formatting | bytes 1474560 | tf_op jit(solution)/shard_map/all_to_all | solution.py:41
  50.4 2.2 %bitcast_reduce_fusion = (f32[90,128]{0,1:T(8,128)S(1)}, f32[128,90,32]{1,2,0:T(8,128)S(1)}) fusion(bf16[128,90,90]{2,1,0:T(8,128)(2,1)S(1)} %copy.18, bf16[4,8,1,1,90,1,1,128]{4,1,0,7,6,5,3,2:T(8,128)(2,1)} %copy.17), kind=kOutput, calls=%fused_computation.4 | convolution fusion | flops 66712320 | bytes 4331520 | tf_op jit(solution)/shard_map/btq,qtf->fbq/dot_general | solution.py:49
  52.6 0.3 fusion
  53.0 2.1 %copy.19 = bf16[90,32,128]{2,1,0:T(8,128)(2,1)} copy(bf16[90,32,128]{0,1,2:T(8,128)(2,1)S(1)} %fusion) | data formatting | bytes 1474560 | tf_op jit(solution)/shard_map/convert_element_type | solution.py:53
  (5 shorter events, 0.0 us)
Async XLA Ops:
  0.0 28.7 %copy-start = (s32[4096]{0:T(1024)S(1)}, s32[4096]{0:T(1024)}, u32[]{:S(2)}) copy-start(s32[4096]{0:T(1024)} %param.6) | copy-start | bytes 49156
  5.4 22.3 %copy-start.2 = (s32[128]{0:T(128)S(1)}, s32[128]{0:T(128)}, u32[]{:S(2)}) copy-start(s32[128]{0:T(128)} %param.5) | copy-start | bytes 1540
  5.5 22.6 %copy-start.1 = (bf16[16,90,90]{2,0,1:T(8,128)(2,1)S(1)}, bf16[16,90,90]{2,0,1:T(8,128)(2,1)}, u32[]{:S(2)}) copy-start(bf16[16,90,90]{2,0,1:T(8,128)(2,1)} %param.7) | copy-start | bytes 777604
  21.9 24.9 %all-to-all-start.1 = ((bf16[4,1,1,90,1,8,128]{6,0,4,3,2,1,5:T(4,128)(2,1)}), bf16[4,1,1,90,1,8,128]{6,0,4,3,2,1,5:T(4,128)(2,1)}, u32[]{:S(2)}, u32[]{:S(2)}) async-start(bf16[4,1,1,90,1,8,128]{6,0,4,3,2,1,5:T(4,128)(2,1)} %copy.16), calls=%async_computation.1 | async-start | bytes 1474560 | tf_op jit(solution)/shard_map/all_to_all | solution.py:41
where the time goes:
time: 55.5 us; the launch traced here: 55.1 us
  local copies, waits for them, and re-layouts  17.6 us (32%)
  blocking collectives  15.3 us (28%)
  waiting for transfers between devices  10.1 us (18%)
  starting transfers between devices  5.83 us (11%)
  matrix products  3.49 us (6%)
  other arithmetic  2.57 us (5%)
    all_to_all x1, blocking collectives, on_device(): lax.all_to_all(shaped, 'ta', split_axis=4, concat_axis=0, tiled=True)  15.3 us
    all_to_all x1, waiting for transfers between devices, on_device(): lax.all_to_all(lax.all_to_all(shaped, 'ta', split_axis=4, concat_axis=0,...  10.1 us
    all_to_all x1, starting transfers between devices, on_device(): lax.all_to_all(lax.all_to_all(shaped, 'ta', split_axis=4, concat_axis=0,...  5.83 us
    reshape x2, local copies, waits for them, and re-layouts, on_device(): per_column.astype(jnp.bfloat16)  5.47 us
    all_to_all x1, local copies, waits for them, and re-layouts, on_device(): lax.all_to_all(lax.all_to_all(shaped, 'ta', split_axis=4, concat_axis=0,...  3.66 us
    dot_general x1, matrix products, on_device(): jnp.einsum('btq,qtf->fbq', gathered, per_column, preferred_element_type=j...  2.16 us
    convert_element_type x1, local copies, waits for them, and re-layouts, on_device(): return (modal_amplitude - mean_coef).astype(jnp.bfloat16)  2.1 us
    unnamed x8, local copies, waits for them, and re-layouts  1.71 us
  transfers between devices with their start and end apart: 1, of which 1 were waited for; matrix products, arithmetic and copies ran while one was open for 16% of the time, Pallas kernels for 0%

commit v1 on v0

v1 whole, which is shorter than its diff:
```python
import functools

import jax
import jax.numpy as jnp
from jax import lax
from jax.experimental import pallas as pl
from jax.experimental.pallas import tpu as pltpu
from jax.sharding import PartitionSpec as P

TILE = 32
MESH = pl.DeviceIdType.MESH
ROWS = 16


def exchange_kernel(
    n_ta, n_tb, col_dev,
    perm_ref, theta_ref, cls_ref, basis_ref,
    coef_ref, total_ref,
    turned_theta, turned_cls, send_buf, recv_buf, basis_rows, basis_t, mask, send_sem, recv_sem,
):
    n = n_ta * n_tb
    ta, tb = lax.axis_index("ta"), lax.axis_index("tb")
    me = ta * n_tb + tb
    _, lev, _ = theta_ref.shape
    classes, _, modes = basis_ref.shape
    pad = recv_buf.shape[1]
    per = col_dev // TILE

    barrier = pltpu.get_barrier_semaphore()

    def greet(k, _):
        other = lax.rem(me + k, n)
        pl.semaphore_signal(
            barrier, inc=1, device_id=(lax.div(other, n_tb), lax.rem(other, n_tb)), device_id_type=MESH
        )
        return 0

    lax.fori_loop(1, n, greet, 0)

    lane_group = lax.broadcasted_iota(jnp.int32, (1, col_dev), 1) // TILE

    def turn(block, _):
        lanes = pl.ds(pl.multiple_of(block * col_dev, col_dev), col_dev)
        piece = theta_ref[0, :, lanes].astype(jnp.float32)
        for k in range(per):
            turned_theta[k, block] = (pltpu.roll(piece, k * TILE, 1) if k else piece).astype(jnp.bfloat16)
        return 0

    lax.fori_loop(0, n, turn, 0)
    for k in range(per):
        turned_cls[k] = pltpu.roll(cls_ref[...], k * TILE, 1) if k else cls_ref[...]

    def regroup(dest, load):
        out = None
        for k in range(per):
            g = perm_ref[dest * per + k]
            shift = lax.rem(k + per - lax.rem(g, per), per)
            piece = load(shift, lax.div(g, per))
            out = piece if out is None else jnp.where(lane_group == k, piece, out)
        return out

    def prepare(dest, _):
        send_buf[dest] = regroup(dest, lambda shift, block: turned_theta[shift, block])
        return 0

    lax.fori_loop(0, n, prepare, 0)
    recv_buf[:, lev:, :] = jnp.zeros((n, pad - lev, col_dev), jnp.bfloat16)
    recv_buf[me, :lev, :] = send_buf[me]

    pl.semaphore_wait(barrier, n - 1)

    def offset(i):
        half = lax.div(i + 1, 2)
        odd = lax.rem(i, 2)
        return lax.rem(n_tb // 2 + odd * half + (1 - odd) * (n_tb - half), n_tb)

    def copy(src, dst, device):
        return pltpu.make_async_remote_copy(
            src_ref=send_buf.at[src],
            dst_ref=recv_buf.at[dst, pl.ds(0, lev), :],
            send_sem=send_sem.at[src],
            recv_sem=recv_sem.at[dst],
            device_id=device,
            device_id_type=MESH,
        )

    def send(i, a):
        to_ta, to_tb = lax.rem(ta + a, n_ta), lax.rem(tb + offset(i), n_tb)
        copy(to_ta * n_tb + to_tb, me, (to_ta, to_tb)).start()

    def send_step(i, _):
        for a in range(n_ta):
            send(i, a)
        return 0

    lax.fori_loop(0, n_tb - 1, send_step, 0)
    for a in range(1, n_ta):
        send(n_tb - 1, a)

    cls = regroup(me, lambda shift, block: turned_cls[shift, pl.ds(block, 1), :])
    for c in range(classes):
        basis_rows[c * pad : c * pad + lev, :] = basis_ref[c]
        basis_rows[c * pad + lev : (c + 1) * pad, :] = jnp.zeros((pad - lev, modes), jnp.bfloat16)
        mask[c] = jnp.broadcast_to((cls == c).astype(jnp.float32), (ROWS, col_dev)).astype(jnp.bfloat16)
    basis_t[...] = jnp.transpose(basis_rows[...])
    total_ref[...] = jnp.zeros_like(total_ref)

    def spread(x):
        x = x.reshape(pad // ROWS, ROWS, col_dev)
        return jnp.concatenate([(x * mask[c][None]).reshape(pad, col_dev) for c in range(classes)], axis=0)

    snaps = n

    def project(first, second):
        stacked = jnp.concatenate([spread(recv_buf[first]), spread(recv_buf[second])], axis=1)
        coef = jnp.dot(basis_t[...], stacked, preferred_element_type=jnp.float32)
        one, two = coef[:, :col_dev], coef[:, col_dev:]
        coef_ref[pl.ds(first, modes, stride=snaps), :] = one
        coef_ref[pl.ds(second, modes, stride=snaps), :] = two
        total_ref[...] += one + two

    def arrive(i, _):
        from_tb = lax.rem(tb + n_tb - offset(i), n_tb)
        for p in range(n_ta // 2):
            pair = [(2 * p + q) * n_tb + from_tb for q in range(2)]
            for src in pair:

                @pl.when(src != me)
                def _():
                    copy(src, src, (ta, tb)).wait_recv()

            project(*pair)
        return 0

    lax.fori_loop(0, n_tb, arrive, 0)

    def sent(k, _):
        dest = lax.rem(me + k, n)
        copy(dest, dest, (ta, tb)).wait_send()
        return 0

    lax.fori_loop(1, n, sent, 0)


def on_device(theta_cube, station_permutation_map, station_bathymetry_group, baroclinic_basis):
    instants, lev, cols = theta_cube.shape
    classes, _, modes = baroclinic_basis.shape
    n_ta = lax.axis_size("ta")
    n_tb = lax.axis_size("tb")
    n = n_ta * n_tb
    col_dev = cols // n
    pad = -(-lev // ROWS) * ROWS
    vmem = pl.BlockSpec(memory_space=pltpu.VMEM)
    coef, total = pl.pallas_call(
        functools.partial(exchange_kernel, n_ta, n_tb, col_dev),
        out_shape=(
            jax.ShapeDtypeStruct((modes * n, col_dev), jnp.float32),
            jax.ShapeDtypeStruct((modes, col_dev), jnp.float32),
        ),
        in_specs=[pl.BlockSpec(memory_space=pltpu.SMEM), vmem, vmem, vmem],
        out_specs=(vmem, vmem),
        scratch_shapes=[
            pltpu.VMEM((col_dev // TILE, n, lev, col_dev), jnp.bfloat16),
            pltpu.VMEM((col_dev // TILE, n, col_dev), jnp.int32),
            pltpu.VMEM((n, lev, col_dev), jnp.bfloat16),
            pltpu.VMEM((n, pad, col_dev), jnp.bfloat16),
            pltpu.VMEM((classes * pad, modes), jnp.bfloat16),
            pltpu.VMEM((modes, classes * pad), jnp.bfloat16),
            pltpu.VMEM((classes, ROWS, col_dev), jnp.bfloat16),
            pltpu.SemaphoreType.DMA((n,)),
            pltpu.SemaphoreType.DMA((n,)),
        ],
        compiler_params=pltpu.CompilerParams(
            collective_id=0, has_side_effects=True, vmem_limit_bytes=(16 if n <= 64 else 60) * 2**20
        ),
    )(
        station_permutation_map,
        theta_cube,
        station_bathymetry_group.reshape(cols // col_dev, col_dev),
        baroclinic_basis,
    )
    coef = coef.reshape(modes, n, col_dev)
    mean = total * (1.0 / n)
    return (coef - mean[:, None, :]).astype(jnp.bfloat16)


def solution(mesh):
    return jax.shard_map(
        on_device,
        mesh=mesh,
        in_specs=(P(("ta", "tb"), None, None), P(), P(), P()),
        out_specs=P(None, None, ("ta", "tb")),
        check_vma=False,
    )
```

time: 55.5 us -> 36.1 us (0.65)
  Pallas kernels: 0 us -> 31.2 us
  blocking collectives: 15.3 us -> 0 us
  local copies, waits for them, and re-layouts: 17.6 us -> 3.59 us
  waiting for transfers between devices: 10.1 us -> 0 us
  starting transfers between devices: 5.83 us -> 0 us
  matrix products: 3.49 us -> 0 us
  other arithmetic: 2.57 us -> 1.1 us
    pallas_call x0 -> x1, Pallas kernels: none -> 31.2 us  [on_device(): pl.pallas_call(functools.partial(exchange_kernel, n_ta, n_tb, col_dev), o...]
    all_to_all x1 -> x0, blocking collectives: 15.3 us -> none  [on_device(): lax.all_to_all(shaped, 'ta', split_axis=4, concat_axis=0, tiled=True)]
    all_to_all x1 -> x0, waiting for transfers between devices: 10.1 us -> none  [on_device(): lax.all_to_all(lax.all_to_all(shaped, 'ta', split_axis=4, concat_axis=0,...]
    reshape x3 -> x0, local copies, waits for them, and re-layouts: 5.97 us -> none  [the longest x2 5.47 us: on_device(): per_column.astype(jnp.bfloat16)]
    all_to_all x1 -> x0, starting transfers between devices: 5.83 us -> none  [on_device(): lax.all_to_all(lax.all_to_all(shaped, 'ta', split_axis=4, concat_axis=0,...]
    all_to_all x2 -> x0, local copies, waits for them, and re-layouts: 4.81 us -> none  [the longest x1 3.66 us: on_device(): lax.all_to_all(lax.all_to_all(shaped, 'ta', split_axis=4, concat_axis=0,...]
    dot_general x2 -> x0, matrix products: 3.49 us -> none  [the longest x1 2.16 us: on_device(): jnp.einsum('btq,qtf->fbq', gathered, per_column, preferred_element_type=j...]
    convert_element_type x1 -> x0, local copies, waits for them, and re-layouts: 2.1 us -> none  [on_device(): return (modal_amplitude - mean_coef).astype(jnp.bfloat16)]
  transfers between devices with their start and end apart: 1 -> 0, of which waited for: 1 -> 0; matrix products, arithmetic and copies ran while one was open for 16% -> 0% of each run, Pallas kernels for 0% -> 0%
where the time goes in v1:
time: 36.1 us; the launch traced here: 35.9 us
  Pallas kernels  31.2 us (86%)
  local copies, waits for them, and re-layouts  3.59 us (10%)
  other arithmetic  1.1 us (3%)
    pallas_call x1, Pallas kernels, on_device(): pl.pallas_call(functools.partial(exchange_kernel, n_ta, n_tb, col_dev), o...  31.2 us
    unnamed x7, local copies, waits for them, and re-layouts  3.59 us
    convert_element_type x1, other arithmetic, on_device(): return (coef - mean[:, None, :]).astype(jnp.bfloat16)  1.1 us

profile of v1, /device:TPU:0, one launch (start us, length us, event | category | flops | bytes accessed | tf_op | source)
XLA Modules:
  0.0 35.9 jit_solution(5062576471365220520)
XLA Ops:
  0.0 1.1 %copy.5.basis_ref = bf16[16,90,90]{2,1,0:T(8,128)(2,1)S(1)} copy(bf16[16,90,90]{2,0,1:T(8,128)(2,1)} %param.7) | data formatting | bytes 518400 | tf_op args[3]
  1.1 0.0 copy-start
  1.1 1.1 %copy-done = bf16[1,90,4096]{2,1,0:T(8,128)(2,1)S(1)} copy-done((bf16[1,90,4096]{2,1,0:T(8,128)(2,1)S(1)}, bf16[1,90,4096]{2,1,0:T(8,128)(2,1)}, u32[]{:S(2)}) %copy-start) | copy-done | bytes 737304
  2.2 0.0 copy-start.1
  2.2 0.7 %copy-done.1 = s32[4096]{0:T(1024)S(1)} copy-done((s32[4096]{0:T(1024)S(1)}, s32[4096]{0:T(1024)}, u32[]{:S(2)}) %copy-start.1) | copy-done | bytes 16408
  2.9 0.0 copy-start.2
  2.9 0.7 %copy-done.2 = s32[128]{0:T(128)S(1)} copy-done((s32[128]{0:T(128)S(1)}, s32[128]{0:T(128)}, u32[]{:S(2)}) %copy-start.2) | copy-done | bytes 536
  3.6 31.2 %shard_map.46 = (f32[2880,128]{1,0:T(8,128)S(1)}, f32[90,128]{1,0:T(8,128)S(1)}) custom-call(s32[128]{0:T(128)S(1)} %copy-done.2, bf16[1,90,4096]{2,1,0:T(8,128)(2,1)S(1)} %copy-done, s32[32,128]{1,0:T(8,128)S(1)} %bitcast.3, bf16[16,90,90]{2,1,0:T(8,128)(2,1)S(1)} %copy.5.basis_ref), custom_call_target="tpu_custom_call" | custom-call | tf_op jit(solution)/shard_map/pallas_call | solution.py:154
  34.8 1.1 %subtract_convert_fusion = bf16[90,32,128]{2,1,0:T(8,128)(2,1)} fusion(f32[90,32,128]{2,1,0:T(8,128)S(1)} %bitcast.2, f32[90,128]{1,0:T(8,128)S(1)} %broadcast_multiply_fusion), kind=kLoop, calls=%fused_computation | loop fusion | flops 737280 | bytes 2257920 | tf_op jit(solution)/shard_map/convert_element_type | solution.py:184
  (1 shorter events, 0.0 us)
Async XLA Ops:
  1.1 1.1 %copy-start = (bf16[1,90,4096]{2,1,0:T(8,128)(2,1)S(1)}, bf16[1,90,4096]{2,1,0:T(8,128)(2,1)}, u32[]{:S(2)}) copy-start(bf16[1,90,4096]{2,1,0:T(8,128)(2,1)} %theta_ref.1) | copy-start | bytes 2211844
  2.2 0.7 %copy-start.1 = (s32[4096]{0:T(1024)S(1)}, s32[4096]{0:T(1024)}, u32[]{:S(2)}) copy-start(s32[4096]{0:T(1024)} %param.6) | copy-start | bytes 49156
  2.9 0.7 %copy-start.2 = (s32[128]{0:T(128)S(1)}, s32[128]{0:T(128)}, u32[]{:S(2)}) copy-start(s32[128]{0:T(128)} %perm_ref.1) | copy-start | bytes 1540

commit v2 on v1

v2 whole, which is shorter than its diff:
```python
import functools

import jax
import jax.numpy as jnp
from jax import lax
from jax.experimental import pallas as pl
from jax.experimental.pallas import tpu as pltpu
from jax.sharding import PartitionSpec as P

TILE = 32
MESH = pl.DeviceIdType.MESH
ROWS = 16


def exchange_kernel(
    n_ta, n_tb, col_dev,
    perm_ref, theta_hbm, cls_hbm, basis_hbm,
    coef_ref, total_ref,
    theta_ref, cls_ref, basis_ref, basis_wide,
    turns, turned_cls, send_buf, recv_buf, basis_rows, basis_t, mask, load_sem, theta_sem, send_sem, recv_sem,
):
    n = n_ta * n_tb
    ta, tb = lax.axis_index("ta"), lax.axis_index("tb")
    me = ta * n_tb + tb
    _, lev, _ = theta_ref.shape
    _, classes, modes = basis_ref.shape
    pad = recv_buf.shape[1]
    per = col_dev // TILE

    def theta_load(block):
        lanes = pl.ds(pl.multiple_of(block * col_dev, col_dev), col_dev)
        return pltpu.make_async_copy(theta_hbm.at[0, :, lanes], theta_ref.at[block], theta_sem.at[block])

    def start_load(block, _):
        theta_load(block).start()
        return 0

    def wait_load(block, _):
        theta_load(block).wait()
        return 0

    cls_load = pltpu.make_async_copy(cls_hbm, cls_ref, load_sem.at[0])
    basis_load = pltpu.make_async_copy(basis_hbm, basis_ref, load_sem.at[1])
    lax.fori_loop(0, n, start_load, 0)
    cls_load.start()
    basis_load.start()

    barrier = pltpu.get_barrier_semaphore()

    def greet(k, _):
        other = lax.rem(me + k, n)
        pl.semaphore_signal(
            barrier, inc=1, device_id=(lax.div(other, n_tb), lax.rem(other, n_tb)), device_id_type=MESH
        )
        return 0

    lax.fori_loop(1, n, greet, 0)


    row = lax.broadcasted_iota(jnp.int32, (col_dev, col_dev), 0)
    lane = lax.broadcasted_iota(jnp.int32, (col_dev, col_dev), 1)
    for s in range(per):
        landed = lax.rem(row + s * TILE, col_dev) == lane
        for k in range(per):
            turns[k, s] = jnp.where(landed & (lane // TILE == k), 1.0, 0.0).astype(jnp.bfloat16)

    def group_place(dest, k):
        g = perm_ref[dest * per + k]
        return lax.div(g, per), lax.rem(k + per - lax.rem(g, per), per)

    def regroup(dest):
        pieces, moves = [], []
        for k in range(per):
            block, shift = group_place(dest, k)
            pieces.append(theta_ref[block])
            moves.append(turns[k, shift])
        return jnp.dot(
            jnp.concatenate(pieces, axis=1), jnp.concatenate(moves, axis=0), preferred_element_type=jnp.float32
        )

    recv_buf[:, lev:, :] = jnp.zeros((n, pad - lev, col_dev), jnp.bfloat16)
    lax.fori_loop(0, n, wait_load, 0)

    def prepare(dest):
        send_buf[dest] = regroup(dest).astype(jnp.bfloat16)

    pl.semaphore_wait(barrier, n - 1)

    def flip(place, by):
        out, bit = 0, 1
        while bit < max(n_ta, n_tb):
            out = out + bit * lax.rem(lax.div(place, bit) + lax.div(by, bit), 2)
            bit *= 2
        return out

    def offset(i):
        return (1 - lax.rem(i, 2)) * (n_tb // 2) + (n_tb // 2 - 1 - lax.div(i, 2))

    def copy(src, dst, device):
        return pltpu.make_async_remote_copy(
            src_ref=send_buf.at[src],
            dst_ref=recv_buf.at[dst, pl.ds(0, lev), :],
            send_sem=send_sem.at[src],
            recv_sem=recv_sem.at[dst],
            device_id=device,
            device_id_type=MESH,
        )

    def target(i, a):
        return flip(ta, a), flip(tb, offset(i))

    def prepare_step(i):
        for a in range(n_ta):
            to_ta, to_tb = target(i, a)
            prepare(to_ta * n_tb + to_tb)

    def send_step(i, first):
        for a in range(first, n_ta):
            to_ta, to_tb = target(i, a)
            copy(to_ta * n_tb + to_tb, me, (to_ta, to_tb)).start()

    prepare_step(0)

    def step(i, _):
        prepare_step(i + 1)
        send_step(i, 0)
        return 0

    lax.fori_loop(0, n_tb - 1, step, 0)
    recv_buf[me, :lev, :] = send_buf[me]
    send_step(n_tb - 1, 1)

    cls_load.wait()
    basis_load.wait()
    basis_wide[...] = basis_ref[...].reshape(lev * classes, modes).astype(jnp.float32)
    for k in range(per):
        turned_cls[k] = pltpu.roll(cls_ref[...], k * TILE, 1) if k else cls_ref[...]
    lane_group = lax.broadcasted_iota(jnp.int32, (1, col_dev), 1) // TILE
    cls = None
    for k in range(per):
        block, shift = group_place(me, k)
        piece = turned_cls[shift, pl.ds(block, 1), :]
        cls = piece if cls is None else jnp.where(lane_group == k, piece, cls)
    for c in range(classes):
        basis_rows[c * pad : c * pad + lev, :] = basis_wide[pl.ds(c, lev, stride=classes), :].astype(jnp.bfloat16)
        basis_rows[c * pad + lev : (c + 1) * pad, :] = jnp.zeros((pad - lev, modes), jnp.bfloat16)
        mask[c] = jnp.broadcast_to((cls == c).astype(jnp.float32), (ROWS, col_dev)).astype(jnp.bfloat16)
    basis_t[...] = jnp.transpose(basis_rows[...])
    total_ref[...] = jnp.zeros_like(total_ref)

    def spread(x):
        x = x.reshape(pad // ROWS, ROWS, col_dev)
        return jnp.concatenate([(x * mask[c][None]).reshape(pad, col_dev) for c in range(classes)], axis=0)

    snaps = n

    def project(first, second):
        stacked = jnp.concatenate([spread(recv_buf[first]), spread(recv_buf[second])], axis=1)
        coef = jnp.dot(basis_t[...], stacked, preferred_element_type=jnp.float32)
        one, two = coef[:, :col_dev], coef[:, col_dev:]
        coef_ref[pl.ds(first, modes, stride=snaps), :] = one
        coef_ref[pl.ds(second, modes, stride=snaps), :] = two
        total_ref[...] += one + two

    def arrive(i, _):
        from_tb = flip(tb, offset(i))
        for p in range(n_ta // 2):
            pair = [(2 * p + q) * n_tb + from_tb for q in range(2)]
            for src in pair:

                @pl.when(src != me)
                def _():
                    copy(src, src, (ta, tb)).wait_recv()

            project(*pair)
        return 0

    lax.fori_loop(0, n_tb, arrive, 0)

    def sent(k, _):
        dest = lax.rem(me + k, n)
        copy(dest, dest, (ta, tb)).wait_send()
        return 0

    lax.fori_loop(1, n, sent, 0)


def on_device(theta_cube, station_permutation_map, station_bathymetry_group, baroclinic_basis):
    instants, lev, cols = theta_cube.shape
    classes, _, modes = baroclinic_basis.shape
    n_ta = lax.axis_size("ta")
    n_tb = lax.axis_size("tb")
    n = n_ta * n_tb
    col_dev = cols // n
    pad = -(-lev // ROWS) * ROWS
    coef_bytes = 5 * (modes + 6) * (n + 1) * col_dev
    coef, total = pl.pallas_call(
        functools.partial(exchange_kernel, n_ta, n_tb, col_dev),
        out_shape=(
            pltpu.VMEM((modes * n, col_dev), jnp.float32),
            pltpu.VMEM((modes, col_dev), jnp.float32),
        ),
        in_specs=[pl.BlockSpec(memory_space=pltpu.SMEM)] + [pl.BlockSpec(memory_space=pltpu.HBM)] * 3,
        out_specs=(pl.BlockSpec(memory_space=pltpu.VMEM),) * 2,
        scratch_shapes=[
            pltpu.VMEM((n, lev, col_dev), jnp.bfloat16),
            pltpu.VMEM((cols // col_dev, col_dev), jnp.int32),
            pltpu.VMEM((lev, classes, modes), jnp.bfloat16),
            pltpu.VMEM((lev * classes, modes), jnp.float32),
            pltpu.VMEM((col_dev // TILE, col_dev // TILE, col_dev, col_dev), jnp.bfloat16),
            pltpu.VMEM((col_dev // TILE, cols // col_dev, col_dev), jnp.int32),
            pltpu.VMEM((n, lev, col_dev), jnp.bfloat16),
            pltpu.VMEM((n, pad, col_dev), jnp.bfloat16),
            pltpu.VMEM((classes * pad, modes), jnp.bfloat16),
            pltpu.VMEM((modes, classes * pad), jnp.bfloat16),
            pltpu.VMEM((classes, ROWS, col_dev), jnp.bfloat16),
            pltpu.SemaphoreType.DMA((2,)),
            pltpu.SemaphoreType.DMA((n,)),
            pltpu.SemaphoreType.DMA((n,)),
            pltpu.SemaphoreType.DMA((n,)),
        ],
        compiler_params=pltpu.CompilerParams(
            collective_id=0, has_side_effects=True, vmem_limit_bytes=67043328 - coef_bytes
        ),
    )(
        station_permutation_map,
        theta_cube,
        station_bathymetry_group.reshape(cols // col_dev, col_dev),
        jnp.transpose(baroclinic_basis, (1, 0, 2)),
    )
    coef = coef.reshape(modes, n, col_dev)
    mean = total * (1.0 / n)
    return (coef - mean[:, None, :]).astype(jnp.bfloat16)


def solution(mesh):
    return jax.shard_map(
        on_device,
        mesh=mesh,
        in_specs=(P(("ta", "tb"), None, None), P(), P(), P()),
        out_specs=P(None, None, ("ta", "tb")),
        check_vma=False,
    )
```

time: 36.1 us -> 29.7 us (0.82)
  local copies, waits for them, and re-layouts: 3.59 us -> 0 us
  Pallas kernels: 31.2 us -> 28.4 us
    unnamed x7 -> x0, local copies, waits for them, and re-layouts: 3.59 us -> none
    pallas_call x1, Pallas kernels: 31.2 us -> 28.4 us  [on_device(): pl.pallas_call(functools.partial(exchange_kernel, n_ta, n_tb, col_dev), o...]
where the time goes in v2:
time: 29.7 us; the launch traced here: 29.5 us
  Pallas kernels  28.4 us (96%)
  other arithmetic  1.1 us (4%)
    pallas_call x1, Pallas kernels, on_device(): pl.pallas_call(functools.partial(exchange_kernel, n_ta, n_tb, col_dev), o...  28.4 us
    convert_element_type x1, other arithmetic, on_device(): return (coef - mean[:, None, :]).astype(jnp.bfloat16)  1.1 us

profile of v2, /device:TPU:0, one launch (start us, length us, event | category | flops | bytes accessed | tf_op | source)
XLA Modules:
  0.0 29.5 jit_solution(10020594566259221035)
XLA Ops:
  0.0 28.4 %shard_map.46 = (f32[2880,128]{1,0:T(8,128)S(1)}, f32[90,128]{1,0:T(8,128)S(1)}) custom-call(s32[128]{0:T(128)} %perm_ref.1, bf16[1,90,4096]{2,1,0:T(8,128)(2,1)} %theta_hbm.1, s32[32,128]{1,0:T(8,128)} %bitcast.5, bf16[90,16,90]{2,1,0:T(8,128)(2,1)} %bitcast.4), custom_call_target="tpu_custom_call" | custom-call | tf_op jit(solution)/shard_map/pallas_call | solution.py:197
  28.4 1.1 %subtract_convert_fusion = bf16[90,32,128]{2,1,0:T(8,128)(2,1)} fusion(f32[90,32,128]{2,1,0:T(8,128)S(1)} %bitcast.3, f32[90,128]{1,0:T(8,128)S(1)} %broadcast_multiply_fusion), kind=kLoop, calls=%fused_computation | loop fusion | flops 737280 | bytes 2257920 | tf_op jit(solution)/shard_map/convert_element_type | solution.py:233
  (1 shorter events, 0.0 us)
